TPU v7x, 32 devices: a whole 2x2x4 slice. The times are simulated.
32 devices in a mesh: seq: 8 (over y, x, core), tensor: 4 (over z).
Axes of the slice: x: 2, y: 2, z: 4, core: 2. Of those that a mesh axis runs over, the one named last changes fastest.
Arguments:
- tokens: bfloat16 [5760, 1536], P('seq'), may hold values from -6 to 6
- norm_gain: float32 [1536], replicated, may hold values from 0.1 to 1.9
- w_qkv: bfloat16 [1536, 3, 1536], P(None, None, 'tensor'), may hold values from -8 to 8
- w_out: bfloat16 [1536, 1536], P('tensor'), may hold values from -0.15625 to 0.15625
- post_gain: float32 [1536], replicated, may hold values from 0.1 to 1.9
- w_up: bfloat16 [1536, 6144], P(None, 'tensor'), may hold values from -0.15625 to 0.15625
- w_down: bfloat16 [6144, 1536], P('tensor'), may hold values from -0.078125 to 0.078125
Outputs:
- layer_out: bfloat16 [5760, 1536], P('seq')
All inputs are finite; a program needn't handle non-finite values.
Results may differ from a plain program's by a relative error of at most 0.015.
Values may be sent and summed in bfloat16 or wider, within the bound.
A program may use at most 128 MiB of HBM per device.

v0:
```python
import jax
import jax.numpy as jnp
from jax import lax
from jax.sharding import PartitionSpec as P

HD = 48


def layer_norm(values, gain):
    mean = jnp.mean(values, axis=-1, keepdims=True)
    centred = values - mean
    var = jnp.mean(centred * centred, axis=-1, keepdims=True)
    return centred * lax.rsqrt(var + 1e-05) * gain


def attend_block(carry, queries, key_rows, value_rows, scale):
    peak, total, accum = carry
    heads = queries.shape[1]
    keys = key_rows.reshape(key_rows.shape[0], heads, -1)
    values = value_rows.reshape(value_rows.shape[0], heads, -1)
    scores = jnp.einsum("qhd,khd->hqk", queries, keys, preferred_element_type=jnp.float32) * scale
    fresh = jnp.maximum(peak, jnp.max(scores, axis=-1))
    factor = jnp.exp(peak - fresh)
    weights = jnp.exp(scores - fresh[..., None])
    total = total * factor + jnp.sum(weights, axis=-1)
    accum = accum * factor[..., None] + jnp.einsum(
        "hqk,khd->hqd", weights.astype(jnp.bfloat16), values, preferred_element_type=jnp.float32
    )
    return (fresh, total, accum)


def empty_state(rows, heads, width):
    return (
        jnp.full((heads, rows), -1e30, jnp.float32),
        jnp.zeros((heads, rows), jnp.float32),
        jnp.zeros((heads, rows, width), jnp.float32),
    )


def per_device(tokens, norm_gain, w_qkv, w_out, post_gain, w_up, w_down):
    rows = tokens.shape[0]
    local_heads = w_qkv.shape[2] // HD
    scale = 1.0 / HD**0.5
    base = tokens.astype(jnp.float32)
    normed = layer_norm(base, norm_gain).astype(jnp.bfloat16)
    qkv = jnp.dot(
        normed, w_qkv.reshape(w_qkv.shape[0], -1), preferred_element_type=jnp.float32
    ).astype(jnp.bfloat16)
    span = local_heads * HD
    query = qkv[:, :span]
    key = qkv[:, span : 2 * span]
    value = qkv[:, 2 * span :]
    query3 = query.reshape(rows, local_heads, HD)
    key_piece = lax.all_gather(key, "seq", axis=0, tiled=True)
    value_piece = lax.all_gather(value, "seq", axis=0, tiled=True)
    count = key_piece.shape[0]
    block = count
    while block > 1024 and block % 2 == 0:
        block = block // 2

    def step(index, state):
        first = index * block
        key_block = lax.dynamic_slice_in_dim(key_piece, first, block, 0)
        value_block = lax.dynamic_slice_in_dim(value_piece, first, block, 0)
        return attend_block(state, query3, key_block, value_block, scale)

    peak, total, accum = lax.fori_loop(0, count // block, step, empty_state(rows, local_heads, HD))
    result = accum / total[..., None]
    attended = jnp.transpose(result, (1, 0, 2)).reshape(rows, span).astype(jnp.bfloat16)
    attn_term = jnp.dot(attended, w_out, preferred_element_type=jnp.float32)
    mixed = base + lax.psum(attn_term.astype(jnp.bfloat16), "tensor").astype(jnp.float32)
    post = layer_norm(mixed, post_gain).astype(jnp.bfloat16)
    hidden = jax.nn.gelu(
        jnp.dot(post, w_up, preferred_element_type=jnp.float32), approximate=True
    ).astype(jnp.bfloat16)
    mlp_term = jnp.dot(hidden, w_down, preferred_element_type=jnp.float32)
    return (mixed + lax.psum(mlp_term.astype(jnp.bfloat16), "tensor").astype(jnp.float32)).astype(
        jnp.bfloat16
    )


def solution(mesh):
    placed = (
        P("seq", None),
        P(),
        P(None, None, "tensor"),
        P("tensor", None),
        P(),
        P(None, "tensor"),
        P("tensor", None),
    )
    return jax.shard_map(
        per_device, mesh=mesh, in_specs=placed, out_specs=P("seq", None), check_vma=False
    )
```

profile of v0, /device:TPU:0, one launch (start us, length us, event | category | flops | bytes accessed | tf_op | source)
XLA Modules:
  0.0 578.7 jit_solution(9343756593150286933)
XLA Ops:
  11.1 6.1 %copy.13 = bf16[1536,3,384]{0,2,1:T(8,128)(2,1)} copy(bf16[1536,3,384]{2,0,1:T(8,128)(2,1)} %param.11) | data formatting | bytes 7077888 | tf_op args[2]
  17.3 5.1 convolution_convert_fusion.2
  24.9 39.2 %all-gather.5.cloned.1.call-done = bf16[5760,384]{1,0:T(8,128)(2,1)} async-done(((bf16[720,384]{1,0:T(8,128)(2,1)}), bf16[5760,384]{1,0:T(8,128)(2,1)}) %all-gather.5.cloned.1.call-update) | async-done | bytes 4423696 | tf_op jit(solution)/shard_map/all_gather | solution.py:55
  64.0 39.5 %all-gather.3.cloned.1.call-done = bf16[5760,384]{1,0:T(8,128)(2,1)} async-done(((bf16[720,384]{1,0:T(8,128)(2,1)}), bf16[5760,384]{1,0:T(8,128)(2,1)}) %all-gather.3.cloned.1.call-update) | async-done | bytes 4423696 | tf_op jit(solution)/shard_map/all_gather | solution.py:54
  103.5 264.1 %while.18 = (s32[]{:T(128)}, f32[8,720]{1,0:T(8,128)}, f32[8,720]{1,0:T(8,128)}, f32[8,720,48]{1,2,0:T(8,128)}, bf16[5760,384]{1,0:T(8,128)(2,1)}, /*index=5*/bf...) while((s32[]{:T(128)}, f32[8,720]{1,0:T(8,128)}, ...), condition=%wide.region_5.0_spmd.clone, body=%wide.region_2.0_spmd.clone.sunk | while | flops 830298240 | bytes 67369216 | solution.py:67
  105.3 8.6 %bitcast_reduce_fusion.2 = (f32[8,720]{1,0:T(8,128)S(1)}, f32[8,720,720]{2,1,0:T(8,128)}) fusion(bf16[720,8,48]{0,2,1:T(8,128)(2,1)S(1)} %bitcast.44, bf16[720,8,48]{0,2,1:T(8,128)(2,1)S(1)} %get-tuple-element.275), kind=kOutput, calls=%fused_computation.1.clone.1 | convolution fusion | flops 406419840 | bytes 17717760 | tf_op jit(solution)/shard_map/while/body/eval_jaxpr/qhd,khd->hqk/dot_general | solution.py:21
  114.5 9.7 %fusion.56 = f32[8,720]{1,0:T(8,128)} fusion(f32[8,720,720]{2,1,0:T(8,128)} %get-tuple-element.244, f32[8,720]{1,0:T(8,128)} %select_maximum_fusion.2), kind=kLoop, calls=%fused_computation.4.clone.1 | loop fusion | flops 12435840 | bytes 16634880 | tf_op jit(solution)/shard_map/while/body/eval_jaxpr/reduce_sum | solution.py:25
  125.6 9.2 %fusion.58 = f32[8,720,48]{1,2,0:T(8,128)S(1)} fusion(bf16[720,8,48]{0,2,1:T(8,128)(2,1)S(1)} %bitcast.43, f32[8,720,720]{2,1,0:T(8,128)} %get-tuple-element.244, f32[8,720]{1,0:T(8,128)} %select_maximum_fusion.2, f32[8,720,48]{1,2,0:T(8,128)S(1)} %copy-done.3, f32[8,720]{1,0:T(8,128)S(1)} %get-tuple-element.247, pred[]{:T(512)S(6)} %compare.3), kind=kOutput, calls=%fused_computation.6.clone.1 | convolution fusion | flops 411402240 | bytes 19399680 | tf_op jit(solution)/shard_map/while/body/eval_jaxpr/hqk,khd->hqd/dot_general | solution.py:26
  137.7 8.6 %bitcast_reduce_fusion.2 = (f32[8,720]{1,0:T(8,128)S(1)}, f32[8,720,720]{2,1,0:T(8,128)}) fusion(bf16[720,8,48]{0,2,1:T(8,128)(2,1)S(1)} %bitcast.44, bf16[720,8,48]{0,2,1:T(8,128)(2,1)S(1)} %get-tuple-element.275), kind=kOutput, calls=%fused_computation.1.clone.1 | convolution fusion | flops 406419840 | bytes 17717760 | tf_op jit(solution)/shard_map/while/body/eval_jaxpr/qhd,khd->hqk/dot_general | solution.py:21
  147.6 9.7 %fusion.56 = f32[8,720]{1,0:T(8,128)} fusion(f32[8,720,720]{2,1,0:T(8,128)} %get-tuple-element.244, f32[8,720]{1,0:T(8,128)} %select_maximum_fusion.2), kind=kLoop, calls=%fused_computation.4.clone.1 | loop fusion | flops 12435840 | bytes 16634880 | tf_op jit(solution)/shard_map/while/body/eval_jaxpr/reduce_sum | solution.py:25
  158.7 9.2 %fusion.58 = f32[8,720,48]{1,2,0:T(8,128)S(1)} fusion(bf16[720,8,48]{0,2,1:T(8,128)(2,1)S(1)} %bitcast.43, f32[8,720,720]{2,1,0:T(8,128)} %get-tuple-element.244, f32[8,720]{1,0:T(8,128)} %select_maximum_fusion.2, f32[8,720,48]{1,2,0:T(8,128)S(1)} %copy-done.3, f32[8,720]{1,0:T(8,128)S(1)} %get-tuple-element.247, pred[]{:T(512)S(6)} %compare.3), kind=kOutput, calls=%fused_computation.6.clone.1 | convolution fusion | flops 411402240 | bytes 19399680 | tf_op jit(solution)/shard_map/while/body/eval_jaxpr/hqk,khd->hqd/dot_general | solution.py:26
  170.8 8.6 %bitcast_reduce_fusion.2 = (f32[8,720]{1,0:T(8,128)S(1)}, f32[8,720,720]{2,1,0:T(8,128)}) fusion(bf16[720,8,48]{0,2,1:T(8,128)(2,1)S(1)} %bitcast.44, bf16[720,8,48]{0,2,1:T(8,128)(2,1)S(1)} %get-tuple-element.275), kind=kOutput, calls=%fused_computation.1.clone.1 | convolution fusion | flops 406419840 | bytes 17717760 | tf_op jit(solution)/shard_map/while/body/eval_jaxpr/qhd,khd->hqk/dot_general | solution.py:21
  180.7 9.7 %fusion.56 = f32[8,720]{1,0:T(8,128)} fusion(f32[8,720,720]{2,1,0:T(8,128)} %get-tuple-element.244, f32[8,720]{1,0:T(8,128)} %select_maximum_fusion.2), kind=kLoop, calls=%fused_computation.4.clone.1 | loop fusion | flops 12435840 | bytes 16634880 | tf_op jit(solution)/shard_map/while/body/eval_jaxpr/reduce_sum | solution.py:25
  191.9 9.2 %fusion.58 = f32[8,720,48]{1,2,0:T(8,128)S(1)} fusion(bf16[720,8,48]{0,2,1:T(8,128)(2,1)S(1)} %bitcast.43, f32[8,720,720]{2,1,0:T(8,128)} %get-tuple-element.244, f32[8,720]{1,0:T(8,128)} %select_maximum_fusion.2, f32[8,720,48]{1,2,0:T(8,128)S(1)} %copy-done.3, f32[8,720]{1,0:T(8,128)S(1)} %get-tuple-element.247, pred[]{:T(512)S(6)} %compare.3), kind=kOutput, calls=%fused_computation.6.clone.1 | convolution fusion | flops 411402240 | bytes 19399680 | tf_op jit(solution)/shard_map/while/body/eval_jaxpr/hqk,khd->hqd/dot_general | solution.py:26
  203.9 8.6 %bitcast_reduce_fusion.2 = (f32[8,720]{1,0:T(8,128)S(1)}, f32[8,720,720]{2,1,0:T(8,128)}) fusion(bf16[720,8,48]{0,2,1:T(8,128)(2,1)S(1)} %bitcast.44, bf16[720,8,48]{0,2,1:T(8,128)(2,1)S(1)} %get-tuple-element.275), kind=kOutput, calls=%fused_computation.1.clone.1 | convolution fusion | flops 406419840 | bytes 17717760 | tf_op jit(solution)/shard_map/while/body/eval_jaxpr/qhd,khd->hqk/dot_general | solution.py:21
  213.8 9.7 %fusion.56 = f32[8,720]{1,0:T(8,128)} fusion(f32[8,720,720]{2,1,0:T(8,128)} %get-tuple-element.244, f32[8,720]{1,0:T(8,128)} %select_maximum_fusion.2), kind=kLoop, calls=%fused_computation.4.clone.1 | loop fusion | flops 12435840 | bytes 16634880 | tf_op jit(solution)/shard_map/while/body/eval_jaxpr/reduce_sum | solution.py:25
  225.0 9.2 %fusion.58 = f32[8,720,48]{1,2,0:T(8,128)S(1)} fusion(bf16[720,8,48]{0,2,1:T(8,128)(2,1)S(1)} %bitcast.43, f32[8,720,720]{2,1,0:T(8,128)} %get-tuple-element.244, f32[8,720]{1,0:T(8,128)} %select_maximum_fusion.2, f32[8,720,48]{1,2,0:T(8,128)S(1)} %copy-done.3, f32[8,720]{1,0:T(8,128)S(1)} %get-tuple-element.247, pred[]{:T(512)S(6)} %compare.3), kind=kOutput, calls=%fused_computation.6.clone.1 | convolution fusion | flops 411402240 | bytes 19399680 | tf_op jit(solution)/shard_map/while/body/eval_jaxpr/hqk,khd->hqd/dot_general | solution.py:26
  237.0 8.6 %bitcast_reduce_fusion.2 = (f32[8,720]{1,0:T(8,128)S(1)}, f32[8,720,720]{2,1,0:T(8,128)}) fusion(bf16[720,8,48]{0,2,1:T(8,128)(2,1)S(1)} %bitcast.44, bf16[720,8,48]{0,2,1:T(8,128)(2,1)S(1)} %get-tuple-element.275), kind=kOutput, calls=%fused_computation.1.clone.1 | convolution fusion | flops 406419840 | bytes 17717760 | tf_op jit(solution)/shard_map/while/body/eval_jaxpr/qhd,khd->hqk/dot_general | solution.py:21
  246.9 9.7 %fusion.56 = f32[8,720]{1,0:T(8,128)} fusion(f32[8,720,720]{2,1,0:T(8,128)} %get-tuple-element.244, f32[8,720]{1,0:T(8,128)} %select_maximum_fusion.2), kind=kLoop, calls=%fused_computation.4.clone.1 | loop fusion | flops 12435840 | bytes 16634880 | tf_op jit(solution)/shard_map/while/body/eval_jaxpr/reduce_sum | solution.py:25
  258.1 9.2 %fusion.58 = f32[8,720,48]{1,2,0:T(8,128)S(1)} fusion(bf16[720,8,48]{0,2,1:T(8,128)(2,1)S(1)} %bitcast.43, f32[8,720,720]{2,1,0:T(8,128)} %get-tuple-element.244, f32[8,720]{1,0:T(8,128)} %select_maximum_fusion.2, f32[8,720,48]{1,2,0:T(8,128)S(1)} %copy-done.3, f32[8,720]{1,0:T(8,128)S(1)} %get-tuple-element.247, pred[]{:T(512)S(6)} %compare.3), kind=kOutput, calls=%fused_computation.6.clone.1 | convolution fusion | flops 411402240 | bytes 19399680 | tf_op jit(solution)/shard_map/while/body/eval_jaxpr/hqk,khd->hqd/dot_general | solution.py:26
  270.1 8.6 %bitcast_reduce_fusion.2 = (f32[8,720]{1,0:T(8,128)S(1)}, f32[8,720,720]{2,1,0:T(8,128)}) fusion(bf16[720,8,48]{0,2,1:T(8,128)(2,1)S(1)} %bitcast.44, bf16[720,8,48]{0,2,1:T(8,128)(2,1)S(1)} %get-tuple-element.275), kind=kOutput, calls=%fused_computation.1.clone.1 | convolution fusion | flops 406419840 | bytes 17717760 | tf_op jit(solution)/shard_map/while/body/eval_jaxpr/qhd,khd->hqk/dot_general | solution.py:21
  280.0 9.7 %fusion.56 = f32[8,720]{1,0:T(8,128)} fusion(f32[8,720,720]{2,1,0:T(8,128)} %get-tuple-element.244, f32[8,720]{1,0:T(8,128)} %select_maximum_fusion.2), kind=kLoop, calls=%fused_computation.4.clone.1 | loop fusion | flops 12435840 | bytes 16634880 | tf_op jit(solution)/shard_map/while/body/eval_jaxpr/reduce_sum | solution.py:25
  291.2 9.2 %fusion.58 = f32[8,720,48]{1,2,0:T(8,128)S(1)} fusion(bf16[720,8,48]{0,2,1:T(8,128)(2,1)S(1)} %bitcast.43, f32[8,720,720]{2,1,0:T(8,128)} %get-tuple-element.244, f32[8,720]{1,0:T(8,128)} %select_maximum_fusion.2, f32[8,720,48]{1,2,0:T(8,128)S(1)} %copy-done.3, f32[8,720]{1,0:T(8,128)S(1)} %get-tuple-element.247, pred[]{:T(512)S(6)} %compare.3), kind=kOutput, calls=%fused_computation.6.clone.1 | convolution fusion | flops 411402240 | bytes 19399680 | tf_op jit(solution)/shard_map/while/body/eval_jaxpr/hqk,khd->hqd/dot_general | solution.py:26
  303.2 8.6 %bitcast_reduce_fusion.2 = (f32[8,720]{1,0:T(8,128)S(1)}, f32[8,720,720]{2,1,0:T(8,128)}) fusion(bf16[720,8,48]{0,2,1:T(8,128)(2,1)S(1)} %bitcast.44, bf16[720,8,48]{0,2,1:T(8,128)(2,1)S(1)} %get-tuple-element.275), kind=kOutput, calls=%fused_computation.1.clone.1 | convolution fusion | flops 406419840 | bytes 17717760 | tf_op jit(solution)/shard_map/while/body/eval_jaxpr/qhd,khd->hqk/dot_general | solution.py:21
  313.1 9.7 %fusion.56 = f32[8,720]{1,0:T(8,128)} fusion(f32[8,720,720]{2,1,0:T(8,128)} %get-tuple-element.244, f32[8,720]{1,0:T(8,128)} %select_maximum_fusion.2), kind=kLoop, calls=%fused_computation.4.clone.1 | loop fusion | flops 12435840 | bytes 16634880 | tf_op jit(solution)/shard_map/while/body/eval_jaxpr/reduce_sum | solution.py:25
  324.3 9.2 %fusion.58 = f32[8,720,48]{1,2,0:T(8,128)S(1)} fusion(bf16[720,8,48]{0,2,1:T(8,128)(2,1)S(1)} %bitcast.43, f32[8,720,720]{2,1,0:T(8,128)} %get-tuple-element.244, f32[8,720]{1,0:T(8,128)} %select_maximum_fusion.2, f32[8,720,48]{1,2,0:T(8,128)S(1)} %copy-done.3, f32[8,720]{1,0:T(8,128)S(1)} %get-tuple-element.247, pred[]{:T(512)S(6)} %compare.3), kind=kOutput, calls=%fused_computation.6.clone.1 | convolution fusion | flops 411402240 | bytes 19399680 | tf_op jit(solution)/shard_map/while/body/eval_jaxpr/hqk,khd->hqd/dot_general | solution.py:26
  336.3 8.6 %bitcast_reduce_fusion.2 = (f32[8,720]{1,0:T(8,128)S(1)}, f32[8,720,720]{2,1,0:T(8,128)}) fusion(bf16[720,8,48]{0,2,1:T(8,128)(2,1)S(1)} %bitcast.44, bf16[720,8,48]{0,2,1:T(8,128)(2,1)S(1)} %get-tuple-element.275), kind=kOutput, calls=%fused_computation.1.clone.1 | convolution fusion | flops 406419840 | bytes 17717760 | tf_op jit(solution)/shard_map/while/body/eval_jaxpr/qhd,khd->hqk/dot_general | solution.py:21
  346.2 9.7 %fusion.56 = f32[8,720]{1,0:T(8,128)} fusion(f32[8,720,720]{2,1,0:T(8,128)} %get-tuple-element.244, f32[8,720]{1,0:T(8,128)} %select_maximum_fusion.2), kind=kLoop, calls=%fused_computation.4.clone.1 | loop fusion | flops 12435840 | bytes 16634880 | tf_op jit(solution)/shard_map/while/body/eval_jaxpr/reduce_sum | solution.py:25
  357.4 9.2 %fusion.58 = f32[8,720,48]{1,2,0:T(8,128)S(1)} fusion(bf16[720,8,48]{0,2,1:T(8,128)(2,1)S(1)} %bitcast.43, f32[8,720,720]{2,1,0:T(8,128)} %get-tuple-element.244, f32[8,720]{1,0:T(8,128)} %select_maximum_fusion.2, f32[8,720,48]{1,2,0:T(8,128)S(1)} %copy-done.3, f32[8,720]{1,0:T(8,128)S(1)} %get-tuple-element.247, pred[]{:T(512)S(6)} %compare.3), kind=kOutput, calls=%fused_computation.6.clone.1 | convolution fusion | flops 411402240 | bytes 19399680 | tf_op jit(solution)/shard_map/while/body/eval_jaxpr/hqk,khd->hqd/dot_general | solution.py:26
  372.0 90.0 %all-reduce.3.cloned.1.call-done = bf16[720,1536]{1,0:T(8,128)(2,1)} async-done(((bf16[720,1536]{1,0:T(8,128)(2,1)}), bf16[720,1536]{1,0:T(8,128)(2,1)}) %all-reduce.3.cloned.1.call-update) | async-done | bytes 2211856 | tf_op jit(solution)/shard_map/psum | solution.py:71
  465.4 12.9 %convolution_convert_fusion = bf16[720,1536]{1,0:T(8,128)(2,1)} fusion(bf16[1536,1536]{1,0:T(8,128)(2,1)} %param.15, bf16[1536,1536]{1,0:T(8,128)(2,1)} %param.14, bf16[720,1536]{1,0:T(8,128)(2,1)} %all-reduce.3.cloned.1.call-done, bf16[720,1536]{1,0:T(8,128)(2,1)S(1)} %copy-done.2, f32[1536]{0:T(1024)S(1)} %copy-done.8, f32[720]{0:T(1024)S(1)} %add_rsqrt_fusion, ...), kind=kOutput, calls=%fused_computation.36 | convolution fusion | flops 6813573120 | bytes 16084608 | tf_op jit(solution)/shard_map/dot_general | solution.py:76
  478.4 89.3 %all-reduce.5.cloned.1.call-done = bf16[720,1536]{1,0:T(8,128)(2,1)} async-done(((bf16[720,1536]{1,0:T(8,128)(2,1)}), bf16[720,1536]{1,0:T(8,128)(2,1)}) %all-reduce.5.cloned.1.call-update) | async-done | bytes 2211856 | tf_op jit(solution)/shard_map/psum | solution.py:77
  (132 shorter events, 63.4 us)
Async XLA Ops:
  6.5 362.4 %copy-start = (bf16[384,1536]{1,0:T(8,128)(2,1)S(1)}, bf16[384,1536]{1,0:T(8,128)(2,1)}, u32[]{:S(2)}) copy-start(bf16[384,1536]{1,0:T(8,128)(2,1)} %param.12) | copy-start | bytes 3538948
  6.5 57.5 %all-gather.5.cloned.1.call-start = ((), (), s32[]{:S(2)}) async-start(), calls=%async_computation.1 | async-start | bytes 4976640 | tf_op jit(solution)/shard_map/all_gather | solution.py:55
  8.6 8.6 %copy-start.1 = (bf16[720,1536]{1,0:T(8,128)(2,1)S(1)}, bf16[720,1536]{1,0:T(8,128)(2,1)}, u32[]{:S(2)}) copy-start(bf16[720,1536]{1,0:T(8,128)(2,1)} %param.9) | copy-start | bytes 6635524
  8.6 8.6 %copy-start.7 = (f32[1536]{0:T(1024)S(1)}, f32[1536]{0:T(1024)}, u32[]{:S(2)}) copy-start(f32[1536]{0:T(1024)} %param.10) | copy-start | bytes 18436
  23.6 79.9 %all-gather.3.cloned.1.call-start = ((), (), s32[]{:S(2)}) async-start(), calls=%async_computation | async-start | bytes 4976640 | tf_op jit(solution)/shard_map/all_gather | solution.py:54
  24.3 437.7 %all-reduce.3.cloned.1.call-start = ((), (), s32[]{:S(2)}) async-start(), calls=%async_computation.2 | async-start | bytes 4423680 | tf_op jit(solution)/shard_map/psum | solution.py:71
  114.5 11.1 %copy-start.3 = (f32[8,720,48]{1,2,0:T(8,128)S(1)}, f32[8,720,48]{1,2,0:T(8,128)}, u32[]{:S(2)}) copy-start(f32[8,720,48]{1,2,0:T(8,128)} %get-tuple-element.262) | copy-start | bytes 3317764 | tf_op jit(solution)/shard_map/while
  125.6 9.2 %copy-start.6 = (f32[8,720]{1,0:T(8,128)S(1)}, f32[8,720]{1,0:T(8,128)}, u32[]{:S(2)}) copy-start(f32[8,720]{1,0:T(8,128)} %select_maximum_fusion.2) | copy-start | bytes 69124 | tf_op jit(solution)/shard_map/while
  134.8 1.0 copy-start.4
  147.6 11.2 %copy-start.3 = (f32[8,720,48]{1,2,0:T(8,128)S(1)}, f32[8,720,48]{1,2,0:T(8,128)}, u32[]{:S(2)}) copy-start(f32[8,720,48]{1,2,0:T(8,128)} %get-tuple-element.262) | copy-start | bytes 3317764 | tf_op jit(solution)/shard_map/while
  158.7 9.2 %copy-start.6 = (f32[8,720]{1,0:T(8,128)S(1)}, f32[8,720]{1,0:T(8,128)}, u32[]{:S(2)}) copy-start(f32[8,720]{1,0:T(8,128)} %select_maximum_fusion.2) | copy-start | bytes 69124 | tf_op jit(solution)/shard_map/while
  167.9 1.0 copy-start.4
  180.7 11.2 %copy-start.3 = (f32[8,720,48]{1,2,0:T(8,128)S(1)}, f32[8,720,48]{1,2,0:T(8,128)}, u32[]{:S(2)}) copy-start(f32[8,720,48]{1,2,0:T(8,128)} %get-tuple-element.262) | copy-start | bytes 3317764 | tf_op jit(solution)/shard_map/while
  191.8 9.2 %copy-start.6 = (f32[8,720]{1,0:T(8,128)S(1)}, f32[8,720]{1,0:T(8,128)}, u32[]{:S(2)}) copy-start(f32[8,720]{1,0:T(8,128)} %select_maximum_fusion.2) | copy-start | bytes 69124 | tf_op jit(solution)/shard_map/while
  213.8 11.2 %copy-start.3 = (f32[8,720,48]{1,2,0:T(8,128)S(1)}, f32[8,720,48]{1,2,0:T(8,128)}, u32[]{:S(2)}) copy-start(f32[8,720,48]{1,2,0:T(8,128)} %get-tuple-element.262) | copy-start | bytes 3317764 | tf_op jit(solution)/shard_map/while
  225.0 9.2 %copy-start.6 = (f32[8,720]{1,0:T(8,128)S(1)}, f32[8,720]{1,0:T(8,128)}, u32[]{:S(2)}) copy-start(f32[8,720]{1,0:T(8,128)} %select_maximum_fusion.2) | copy-start | bytes 69124 | tf_op jit(solution)/shard_map/while
  246.9 11.2 %copy-start.3 = (f32[8,720,48]{1,2,0:T(8,128)S(1)}, f32[8,720,48]{1,2,0:T(8,128)}, u32[]{:S(2)}) copy-start(f32[8,720,48]{1,2,0:T(8,128)} %get-tuple-element.262) | copy-start | bytes 3317764 | tf_op jit(solution)/shard_map/while
  258.1 9.2 %copy-start.6 = (f32[8,720]{1,0:T(8,128)S(1)}, f32[8,720]{1,0:T(8,128)}, u32[]{:S(2)}) copy-start(f32[8,720]{1,0:T(8,128)} %select_maximum_fusion.2) | copy-start | bytes 69124 | tf_op jit(solution)/shard_map/while
  267.2 1.0 copy-start.4
  280.0 11.2 %copy-start.3 = (f32[8,720,48]{1,2,0:T(8,128)S(1)}, f32[8,720,48]{1,2,0:T(8,128)}, u32[]{:S(2)}) copy-start(f32[8,720,48]{1,2,0:T(8,128)} %get-tuple-element.262) | copy-start | bytes 3317764 | tf_op jit(solution)/shard_map/while
  291.2 9.2 %copy-start.6 = (f32[8,720]{1,0:T(8,128)S(1)}, f32[8,720]{1,0:T(8,128)}, u32[]{:S(2)}) copy-start(f32[8,720]{1,0:T(8,128)} %select_maximum_fusion.2) | copy-start | bytes 69124 | tf_op jit(solution)/shard_map/while
  300.4 1.0 copy-start.4
  313.1 11.2 %copy-start.3 = (f32[8,720,48]{1,2,0:T(8,128)S(1)}, f32[8,720,48]{1,2,0:T(8,128)}, u32[]{:S(2)}) copy-start(f32[8,720,48]{1,2,0:T(8,128)} %get-tuple-element.262) | copy-start | bytes 3317764 | tf_op jit(solution)/shard_map/while
  324.3 9.2 %copy-start.6 = (f32[8,720]{1,0:T(8,128)S(1)}, f32[8,720]{1,0:T(8,128)}, u32[]{:S(2)}) copy-start(f32[8,720]{1,0:T(8,128)} %select_maximum_fusion.2) | copy-start | bytes 69124 | tf_op jit(solution)/shard_map/while
  333.5 1.0 copy-start.4
  346.2 11.2 %copy-start.3 = (f32[8,720,48]{1,2,0:T(8,128)S(1)}, f32[8,720,48]{1,2,0:T(8,128)}, u32[]{:S(2)}) copy-start(f32[8,720,48]{1,2,0:T(8,128)} %get-tuple-element.262) | copy-start | bytes 3317764 | tf_op jit(solution)/shard_map/while
  357.4 9.2 %copy-start.6 = (f32[8,720]{1,0:T(8,128)S(1)}, f32[8,720]{1,0:T(8,128)}, u32[]{:S(2)}) copy-start(f32[8,720]{1,0:T(8,128)} %select_maximum_fusion.2) | copy-start | bytes 69124 | tf_op jit(solution)/shard_map/while
  366.6 1.0 copy-start.4
  369.0 93.0 %copy-start.2 = (bf16[720,1536]{1,0:T(8,128)(2,1)S(1)}, bf16[720,1536]{1,0:T(8,128)(2,1)}, u32[]{:S(2)}) copy-start(bf16[720,1536]{1,0:T(8,128)(2,1)} %param.9) | copy-start | bytes 6635524
  371.7 93.7 %copy-start.8 = (f32[1536]{0:T(1024)S(1)}, f32[1536]{0:T(1024)}, u32[]{:S(2)}) copy-start(f32[1536]{0:T(1024)} %param.13) | copy-start | bytes 18436
  371.7 196.0 %all-reduce.5.cloned.1.call-start = ((), (), s32[]{:S(2)}) async-start(), calls=%async_computation.3 | async-start | bytes 4423680 | tf_op jit(solution)/shard_map/psum | solution.py:77
  462.0 2.4 copy-start.5
  (2 other events, 2.0 us)
Sparse Core Ops, SparseCore 0:
  23.7 40.2 all-gather.4
  65.9 37.5 all-gather.2
  371.8 90.1 all-reduce.2
  478.5 89.1 all-reduce.4
where the time goes:
time: 580 us; the launch traced here: 579 us
  waiting for transfers between devices  259 us (45%)
  matrix products  163 us (28%)
  other arithmetic  113 us (19%)
  local copies, waits for them, and re-layouts  30.3 us (5%)
  between operations  13.2 us (2%)
    psum x1, waiting for transfers between devices, per_device(): lax.psum(attn_term.astype(jnp.bfloat16), 'tensor').astype(jnp.float32)  90 us
    psum x1, waiting for transfers between devices, per_device(): lax.psum(mlp_term.astype(jnp.bfloat16), 'tensor').astype(jnp.float32)  89.3 us
    reduce_sum x8, other arithmetic, attend_block(): total = total * factor + jnp.sum(weights, axis=-1)  77.9 us
    dot_general x8, matrix products, attend_block(): jnp.einsum('hqk,khd->hqd', weights.astype(jnp.bfloat16), values, preferre...  73.3 us
    dot_general x8, matrix products, attend_block(): jnp.einsum('qhd,khd->hqk', queries, keys, preferred_element_type=jnp.floa...  68.5 us
    all_gather x1, waiting for transfers between devices, per_device(): key_piece = lax.all_gather(key, 'seq', axis=0, tiled=True)  39.5 us
    all_gather x1, waiting for transfers between devices, per_device(): value_piece = lax.all_gather(value, 'seq', axis=0, tiled=True)  39.2 us
    dot_general x1, matrix products, per_device(): mlp_term = jnp.dot(hidden, w_down, preferred_element_type=jnp.float32)  12.9 us
  transfers between devices with their start and end apart: 4, of which 4 were waited for; matrix products, arithmetic and copies ran while one was open for 0% of the time, Pallas kernels for 0%

commit v1 on v0

--- a/solution.py
+++ b/solution.py
@@ -1,9 +1,18 @@
+import functools
 import jax
 import jax.numpy as jnp
 from jax import lax
 from jax.sharding import PartitionSpec as P
 
 HD = 48
+
+
+def change_skins(arr, axis_id):
+    reached = lax.all_gather(arr, axis_id)
+    return jnp.sum(reached, 0)
+
+
+load_shards = functools.partial(change_skins, axis_id="tensor")
 
 
 def layer_norm(values, gain):
@@ -74,7 +83,7 @@
         jnp.dot(post, w_up, preferred_element_type=jnp.float32), approximate=True
     ).astype(jnp.bfloat16)
     mlp_term = jnp.dot(hidden, w_down, preferred_element_type=jnp.float32)
-    return (mixed + lax.psum(mlp_term.astype(jnp.bfloat16), "tensor").astype(jnp.float32)).astype(
+    return (mixed + load_shards(mlp_term.astype(jnp.bfloat16)).astype(jnp.float32)).astype(
         jnp.bfloat16
     )
 

time: 580 us -> 654 us (1.13)
  waiting for transfers between devices: 259 us -> 326 us
  other arithmetic: 113 us -> 120 us
    all_gather x0 -> x1, waiting for transfers between devices: none -> 156 us  [change_skins(): reached = lax.all_gather(arr, axis_id)]
    psum x1 -> x0, waiting for transfers between devices: 89.3 us -> none  [per_device(): lax.psum(mlp_term.astype(jnp.bfloat16), 'tensor').astype(jnp.float32)]
    reduce_sum x0 -> x1, other arithmetic: none -> 6.89 us  [change_skins(): return jnp.sum(reached, 0)]
where the time goes in v1:
time: 654 us; the launch traced here: 653 us
  waiting for transfers between devices  326 us (50%)
  matrix products  163 us (25%)
  other arithmetic  120 us (18%)
  local copies, waits for them, and re-layouts  30.3 us (5%)
  between operations  13.2 us (2%)
    all_gather x1, waiting for transfers between devices, change_skins(): reached = lax.all_gather(arr, axis_id)  156 us
    psum x1, waiting for transfers between devices, per_device(): lax.psum(attn_term.astype(jnp.bfloat16), 'tensor').astype(jnp.float32)  90 us
    reduce_sum x8, other arithmetic, attend_block(): total = total * factor + jnp.sum(weights, axis=-1)  77.9 us
    dot_general x8, matrix products, attend_block(): jnp.einsum('hqk,khd->hqd', weights.astype(jnp.bfloat16), values, preferre...  73.3 us
    dot_general x8, matrix products, attend_block(): jnp.einsum('qhd,khd->hqk', queries, keys, preferred_element_type=jnp.floa...  68.5 us
    all_gather x1, waiting for transfers between devices, per_device(): key_piece = lax.all_gather(key, 'seq', axis=0, tiled=True)  39.5 us
    all_gather x1, waiting for transfers between devices, per_device(): value_piece = lax.all_gather(value, 'seq', axis=0, tiled=True)  39.2 us
  transfers between devices with their start and end apart: 4, of which 4 were waited for; matrix products, arithmetic and copies ran while one was open for 0% of the time, Pallas kernels for 0%

profile of v1, /device:TPU:0, one launch (start us, length us, event | category | flops | bytes accessed | tf_op | source)
XLA Modules:
  0.0 652.6 jit_solution(15249648961055495076)
XLA Ops:
  11.1 6.1 copy.13
  24.9 39.2 %all-gather.7.cloned.1.call-done = bf16[5760,384]{1,0:T(8,128)(2,1)} async-done(((bf16[720,384]{1,0:T(8,128)(2,1)}), bf16[5760,384]{1,0:T(8,128)(2,1)}) %all-gather.7.cloned.1.call-update) | async-done | bytes 4423696 | tf_op jit(solution)/shard_map/all_gather | solution.py:64
  64.0 39.5 %all-gather.5.cloned.1.call-done = bf16[5760,384]{1,0:T(8,128)(2,1)} async-done(((bf16[720,384]{1,0:T(8,128)(2,1)}), bf16[5760,384]{1,0:T(8,128)(2,1)}) %all-gather.5.cloned.1.call-update) | async-done | bytes 4423696 | tf_op jit(solution)/shard_map/all_gather | solution.py:63
  103.5 264.1 %while.18 = (s32[]{:T(128)}, f32[8,720]{1,0:T(8,128)}, f32[8,720]{1,0:T(8,128)}, f32[8,720,48]{1,2,0:T(8,128)}, bf16[5760,384]{1,0:T(8,128)(2,1)}, /*index=5*/bf...) while((s32[]{:T(128)}, f32[8,720]{1,0:T(8,128)}, ...), condition=%wide.region_5.0_spmd.clone, body=%wide.region_2.0_spmd.clone.sunk | while | flops 830298240 | bytes 67369216 | solution.py:76
  105.3 8.6 %bitcast_reduce_fusion.2 = (f32[8,720]{1,0:T(8,128)S(1)}, f32[8,720,720]{2,1,0:T(8,128)}) fusion(bf16[720,8,48]{0,2,1:T(8,128)(2,1)S(1)} %bitcast.45, bf16[720,8,48]{0,2,1:T(8,128)(2,1)S(1)} %get-tuple-element.275), kind=kOutput, calls=%fused_computation.1.clone.1 | convolution fusion | flops 406419840 | bytes 17717760 | tf_op jit(solution)/shard_map/while/body/eval_jaxpr/qhd,khd->hqk/dot_general | solution.py:30
  114.5 9.7 %fusion.56 = f32[8,720]{1,0:T(8,128)} fusion(f32[8,720,720]{2,1,0:T(8,128)} %get-tuple-element.244, f32[8,720]{1,0:T(8,128)} %select_maximum_fusion.2), kind=kLoop, calls=%fused_computation.4.clone.1 | loop fusion | flops 12435840 | bytes 16634880 | tf_op jit(solution)/shard_map/while/body/eval_jaxpr/reduce_sum | solution.py:34
  125.6 9.2 %fusion.58 = f32[8,720,48]{1,2,0:T(8,128)S(1)} fusion(bf16[720,8,48]{0,2,1:T(8,128)(2,1)S(1)} %bitcast.44, f32[8,720,720]{2,1,0:T(8,128)} %get-tuple-element.244, f32[8,720]{1,0:T(8,128)} %select_maximum_fusion.2, f32[8,720,48]{1,2,0:T(8,128)S(1)} %copy-done.3, f32[8,720]{1,0:T(8,128)S(1)} %get-tuple-element.247, pred[]{:T(512)S(6)} %compare.3), kind=kOutput, calls=%fused_computation.6.clone.1 | convolution fusion | flops 411402240 | bytes 19399680 | tf_op jit(solution)/shard_map/while/body/eval_jaxpr/hqk,khd->hqd/dot_general | solution.py:35
  137.7 8.6 %bitcast_reduce_fusion.2 = (f32[8,720]{1,0:T(8,128)S(1)}, f32[8,720,720]{2,1,0:T(8,128)}) fusion(bf16[720,8,48]{0,2,1:T(8,128)(2,1)S(1)} %bitcast.45, bf16[720,8,48]{0,2,1:T(8,128)(2,1)S(1)} %get-tuple-element.275), kind=kOutput, calls=%fused_computation.1.clone.1 | convolution fusion | flops 406419840 | bytes 17717760 | tf_op jit(solution)/shard_map/while/body/eval_jaxpr/qhd,khd->hqk/dot_general | solution.py:30
  147.6 9.7 %fusion.56 = f32[8,720]{1,0:T(8,128)} fusion(f32[8,720,720]{2,1,0:T(8,128)} %get-tuple-element.244, f32[8,720]{1,0:T(8,128)} %select_maximum_fusion.2), kind=kLoop, calls=%fused_computation.4.clone.1 | loop fusion | flops 12435840 | bytes 16634880 | tf_op jit(solution)/shard_map/while/body/eval_jaxpr/reduce_sum | solution.py:34
  158.7 9.2 %fusion.58 = f32[8,720,48]{1,2,0:T(8,128)S(1)} fusion(bf16[720,8,48]{0,2,1:T(8,128)(2,1)S(1)} %bitcast.44, f32[8,720,720]{2,1,0:T(8,128)} %get-tuple-element.244, f32[8,720]{1,0:T(8,128)} %select_maximum_fusion.2, f32[8,720,48]{1,2,0:T(8,128)S(1)} %copy-done.3, f32[8,720]{1,0:T(8,128)S(1)} %get-tuple-element.247, pred[]{:T(512)S(6)} %compare.3), kind=kOutput, calls=%fused_computation.6.clone.1 | convolution fusion | flops 411402240 | bytes 19399680 | tf_op jit(solution)/shard_map/while/body/eval_jaxpr/hqk,khd->hqd/dot_general | solution.py:35
  170.8 8.6 %bitcast_reduce_fusion.2 = (f32[8,720]{1,0:T(8,128)S(1)}, f32[8,720,720]{2,1,0:T(8,128)}) fusion(bf16[720,8,48]{0,2,1:T(8,128)(2,1)S(1)} %bitcast.45, bf16[720,8,48]{0,2,1:T(8,128)(2,1)S(1)} %get-tuple-element.275), kind=kOutput, calls=%fused_computation.1.clone.1 | convolution fusion | flops 406419840 | bytes 17717760 | tf_op jit(solution)/shard_map/while/body/eval_jaxpr/qhd,khd->hqk/dot_general | solution.py:30
  180.7 9.7 %fusion.56 = f32[8,720]{1,0:T(8,128)} fusion(f32[8,720,720]{2,1,0:T(8,128)} %get-tuple-element.244, f32[8,720]{1,0:T(8,128)} %select_maximum_fusion.2), kind=kLoop, calls=%fused_computation.4.clone.1 | loop fusion | flops 12435840 | bytes 16634880 | tf_op jit(solution)/shard_map/while/body/eval_jaxpr/reduce_sum | solution.py:34
  191.9 9.2 %fusion.58 = f32[8,720,48]{1,2,0:T(8,128)S(1)} fusion(bf16[720,8,48]{0,2,1:T(8,128)(2,1)S(1)} %bitcast.44, f32[8,720,720]{2,1,0:T(8,128)} %get-tuple-element.244, f32[8,720]{1,0:T(8,128)} %select_maximum_fusion.2, f32[8,720,48]{1,2,0:T(8,128)S(1)} %copy-done.3, f32[8,720]{1,0:T(8,128)S(1)} %get-tuple-element.247, pred[]{:T(512)S(6)} %compare.3), kind=kOutput, calls=%fused_computation.6.clone.1 | convolution fusion | flops 411402240 | bytes 19399680 | tf_op jit(solution)/shard_map/while/body/eval_jaxpr/hqk,khd->hqd/dot_general | solution.py:35
  203.9 8.6 %bitcast_reduce_fusion.2 = (f32[8,720]{1,0:T(8,128)S(1)}, f32[8,720,720]{2,1,0:T(8,128)}) fusion(bf16[720,8,48]{0,2,1:T(8,128)(2,1)S(1)} %bitcast.45, bf16[720,8,48]{0,2,1:T(8,128)(2,1)S(1)} %get-tuple-element.275), kind=kOutput, calls=%fused_computation.1.clone.1 | convolution fusion | flops 406419840 | bytes 17717760 | tf_op jit(solution)/shard_map/while/body/eval_jaxpr/qhd,khd->hqk/dot_general | solution.py:30
  213.8 9.7 %fusion.56 = f32[8,720]{1,0:T(8,128)} fusion(f32[8,720,720]{2,1,0:T(8,128)} %get-tuple-element.244, f32[8,720]{1,0:T(8,128)} %select_maximum_fusion.2), kind=kLoop, calls=%fused_computation.4.clone.1 | loop fusion | flops 12435840 | bytes 16634880 | tf_op jit(solution)/shard_map/while/body/eval_jaxpr/reduce_sum | solution.py:34
  225.0 9.2 %fusion.58 = f32[8,720,48]{1,2,0:T(8,128)S(1)} fusion(bf16[720,8,48]{0,2,1:T(8,128)(2,1)S(1)} %bitcast.44, f32[8,720,720]{2,1,0:T(8,128)} %get-tuple-element.244, f32[8,720]{1,0:T(8,128)} %select_maximum_fusion.2, f32[8,720,48]{1,2,0:T(8,128)S(1)} %copy-done.3, f32[8,720]{1,0:T(8,128)S(1)} %get-tuple-element.247, pred[]{:T(512)S(6)} %compare.3), kind=kOutput, calls=%fused_computation.6.clone.1 | convolution fusion | flops 411402240 | bytes 19399680 | tf_op jit(solution)/shard_map/while/body/eval_jaxpr/hqk,khd->hqd/dot_general | solution.py:35
  237.0 8.6 %bitcast_reduce_fusion.2 = (f32[8,720]{1,0:T(8,128)S(1)}, f32[8,720,720]{2,1,0:T(8,128)}) fusion(bf16[720,8,48]{0,2,1:T(8,128)(2,1)S(1)} %bitcast.45, bf16[720,8,48]{0,2,1:T(8,128)(2,1)S(1)} %get-tuple-element.275), kind=kOutput, calls=%fused_computation.1.clone.1 | convolution fusion | flops 406419840 | bytes 17717760 | tf_op jit(solution)/shard_map/while/body/eval_jaxpr/qhd,khd->hqk/dot_general | solution.py:30
  246.9 9.7 %fusion.56 = f32[8,720]{1,0:T(8,128)} fusion(f32[8,720,720]{2,1,0:T(8,128)} %get-tuple-element.244, f32[8,720]{1,0:T(8,128)} %select_maximum_fusion.2), kind=kLoop, calls=%fused_computation.4.clone.1 | loop fusion | flops 12435840 | bytes 16634880 | tf_op jit(solution)/shard_map/while/body/eval_jaxpr/reduce_sum | solution.py:34
  258.1 9.2 %fusion.58 = f32[8,720,48]{1,2,0:T(8,128)S(1)} fusion(bf16[720,8,48]{0,2,1:T(8,128)(2,1)S(1)} %bitcast.44, f32[8,720,720]{2,1,0:T(8,128)} %get-tuple-element.244, f32[8,720]{1,0:T(8,128)} %select_maximum_fusion.2, f32[8,720,48]{1,2,0:T(8,128)S(1)} %copy-done.3, f32[8,720]{1,0:T(8,128)S(1)} %get-tuple-element.247, pred[]{:T(512)S(6)} %compare.3), kind=kOutput, calls=%fused_computation.6.clone.1 | convolution fusion | flops 411402240 | bytes 19399680 | tf_op jit(solution)/shard_map/while/body/eval_jaxpr/hqk,khd->hqd/dot_general | solution.py:35
  270.1 8.6 %bitcast_reduce_fusion.2 = (f32[8,720]{1,0:T(8,128)S(1)}, f32[8,720,720]{2,1,0:T(8,128)}) fusion(bf16[720,8,48]{0,2,1:T(8,128)(2,1)S(1)} %bitcast.45, bf16[720,8,48]{0,2,1:T(8,128)(2,1)S(1)} %get-tuple-element.275), kind=kOutput, calls=%fused_computation.1.clone.1 | convolution fusion | flops 406419840 | bytes 17717760 | tf_op jit(solution)/shard_map/while/body/eval_jaxpr/qhd,khd->hqk/dot_general | solution.py:30
  280.0 9.7 %fusion.56 = f32[8,720]{1,0:T(8,128)} fusion(f32[8,720,720]{2,1,0:T(8,128)} %get-tuple-element.244, f32[8,720]{1,0:T(8,128)} %select_maximum_fusion.2), kind=kLoop, calls=%fused_computation.4.clone.1 | loop fusion | flops 12435840 | bytes 16634880 | tf_op jit(solution)/shard_map/while/body/eval_jaxpr/reduce_sum | solution.py:34
  291.2 9.2 %fusion.58 = f32[8,720,48]{1,2,0:T(8,128)S(1)} fusion(bf16[720,8,48]{0,2,1:T(8,128)(2,1)S(1)} %bitcast.44, f32[8,720,720]{2,1,0:T(8,128)} %get-tuple-element.244, f32[8,720]{1,0:T(8,128)} %select_maximum_fusion.2, f32[8,720,48]{1,2,0:T(8,128)S(1)} %copy-done.3, f32[8,720]{1,0:T(8,128)S(1)} %get-tuple-element.247, pred[]{:T(512)S(6)} %compare.3), kind=kOutput, calls=%fused_computation.6.clone.1 | convolution fusion | flops 411402240 | bytes 19399680 | tf_op jit(solution)/shard_map/while/body/eval_jaxpr/hqk,khd->hqd/dot_general | solution.py:35
  303.2 8.6 %bitcast_reduce_fusion.2 = (f32[8,720]{1,0:T(8,128)S(1)}, f32[8,720,720]{2,1,0:T(8,128)}) fusion(bf16[720,8,48]{0,2,1:T(8,128)(2,1)S(1)} %bitcast.45, bf16[720,8,48]{0,2,1:T(8,128)(2,1)S(1)} %get-tuple-element.275), kind=kOutput, calls=%fused_computation.1.clone.1 | convolution fusion | flops 406419840 | bytes 17717760 | tf_op jit(solution)/shard_map/while/body/eval_jaxpr/qhd,khd->hqk/dot_general | solution.py:30
  313.1 9.7 %fusion.56 = f32[8,720]{1,0:T(8,128)} fusion(f32[8,720,720]{2,1,0:T(8,128)} %get-tuple-element.244, f32[8,720]{1,0:T(8,128)} %select_maximum_fusion.2), kind=kLoop, calls=%fused_computation.4.clone.1 | loop fusion | flops 12435840 | bytes 16634880 | tf_op jit(solution)/shard_map/while/body/eval_jaxpr/reduce_sum | solution.py:34
  324.3 9.2 %fusion.58 = f32[8,720,48]{1,2,0:T(8,128)S(1)} fusion(bf16[720,8,48]{0,2,1:T(8,128)(2,1)S(1)} %bitcast.44, f32[8,720,720]{2,1,0:T(8,128)} %get-tuple-element.244, f32[8,720]{1,0:T(8,128)} %select_maximum_fusion.2, f32[8,720,48]{1,2,0:T(8,128)S(1)} %copy-done.3, f32[8,720]{1,0:T(8,128)S(1)} %get-tuple-element.247, pred[]{:T(512)S(6)} %compare.3), kind=kOutput, calls=%fused_computation.6.clone.1 | convolution fusion | flops 411402240 | bytes 19399680 | tf_op jit(solution)/shard_map/while/body/eval_jaxpr/hqk,khd->hqd/dot_general | solution.py:35
  336.3 8.6 %bitcast_reduce_fusion.2 = (f32[8,720]{1,0:T(8,128)S(1)}, f32[8,720,720]{2,1,0:T(8,128)}) fusion(bf16[720,8,48]{0,2,1:T(8,128)(2,1)S(1)} %bitcast.45, bf16[720,8,48]{0,2,1:T(8,128)(2,1)S(1)} %get-tuple-element.275), kind=kOutput, calls=%fused_computation.1.clone.1 | convolution fusion | flops 406419840 | bytes 17717760 | tf_op jit(solution)/shard_map/while/body/eval_jaxpr/qhd,khd->hqk/dot_general | solution.py:30
  346.2 9.7 %fusion.56 = f32[8,720]{1,0:T(8,128)} fusion(f32[8,720,720]{2,1,0:T(8,128)} %get-tuple-element.244, f32[8,720]{1,0:T(8,128)} %select_maximum_fusion.2), kind=kLoop, calls=%fused_computation.4.clone.1 | loop fusion | flops 12435840 | bytes 16634880 | tf_op jit(solution)/shard_map/while/body/eval_jaxpr/reduce_sum | solution.py:34
  357.4 9.2 %fusion.58 = f32[8,720,48]{1,2,0:T(8,128)S(1)} fusion(bf16[720,8,48]{0,2,1:T(8,128)(2,1)S(1)} %bitcast.44, f32[8,720,720]{2,1,0:T(8,128)} %get-tuple-element.244, f32[8,720]{1,0:T(8,128)} %select_maximum_fusion.2, f32[8,720,48]{1,2,0:T(8,128)S(1)} %copy-done.3, f32[8,720]{1,0:T(8,128)S(1)} %get-tuple-element.247, pred[]{:T(512)S(6)} %compare.3), kind=kOutput, calls=%fused_computation.6.clone.1 | convolution fusion | flops 411402240 | bytes 19399680 | tf_op jit(solution)/shard_map/while/body/eval_jaxpr/hqk,khd->hqd/dot_general | solution.py:35
  372.0 90.0 %all-reduce.2.cloned.1.call-done = bf16[720,1536]{1,0:T(8,128)(2,1)} async-done(((bf16[720,1536]{1,0:T(8,128)(2,1)}), bf16[720,1536]{1,0:T(8,128)(2,1)}) %all-reduce.2.cloned.1.call-update) | async-done | bytes 2211856 | tf_op jit(solution)/shard_map/psum | solution.py:80
  465.4 12.9 %convolution_convert_fusion = bf16[720,1536]{1,0:T(8,128)(2,1)} fusion(bf16[1536,1536]{1,0:T(8,128)(2,1)} %param.15, bf16[1536,1536]{1,0:T(8,128)(2,1)} %param.14, bf16[720,1536]{1,0:T(8,128)(2,1)} %all-reduce.2.cloned.1.call-done, bf16[720,1536]{1,0:T(8,128)(2,1)S(1)} %copy-done.2, f32[1536]{0:T(1024)S(1)} %copy-done.8, f32[720]{0:T(1024)S(1)} %add_rsqrt_fusion, ...), kind=kOutput, calls=%fused_computation.36 | convolution fusion | flops 6813573120 | bytes 16084608 | tf_op jit(solution)/shard_map/dot_general | solution.py:85
  478.4 156.3 %all-gather.9.cloned.1.call-done = bf16[2880,1536]{1,0:T(8,128)(2,1)} async-done(((bf16[720,1536]{1,0:T(8,128)(2,1)}), bf16[2880,1536]{1,0:T(8,128)(2,1)}) %all-gather.9.cloned.1.call-update) | async-done | bytes 8847376 | tf_op jit(solution)/shard_map/all_gather | solution.py:11
  634.7 6.9 %reduce_sum.65 = bf16[720,1536]{1,0:T(8,128)(2,1)} reduce(bf16[4,720,1536]{2,1,0:T(8,128)(2,1)} %bitcast.47, bf16[]{:T(256)} %constant.71.clone.1), dimensions={0}, to_apply=%region_9.0 | reduce | flops 3317760 | bytes 11059202 | tf_op jit(solution)/shard_map/reduce_sum | solution.py:12
  (133 shorter events, 68.5 us)
Async XLA Ops:
  6.5 362.4 %copy-start = (bf16[384,1536]{1,0:T(8,128)(2,1)S(1)}, bf16[384,1536]{1,0:T(8,128)(2,1)}, u32[]{:S(2)}) copy-start(bf16[384,1536]{1,0:T(8,128)(2,1)} %param.12) | copy-start | bytes 3538948
  6.5 57.5 %all-gather.7.cloned.1.call-start = ((), (), s32[]{:S(2)}) async-start(), calls=%async_computation.1 | async-start | bytes 4976640 | tf_op jit(solution)/shard_map/all_gather | solution.py:64
  8.6 8.6 %copy-start.1 = (bf16[720,1536]{1,0:T(8,128)(2,1)S(1)}, bf16[720,1536]{1,0:T(8,128)(2,1)}, u32[]{:S(2)}) copy-start(bf16[720,1536]{1,0:T(8,128)(2,1)} %param.9) | copy-start | bytes 6635524
  8.6 8.6 %copy-start.7 = (f32[1536]{0:T(1024)S(1)}, f32[1536]{0:T(1024)}, u32[]{:S(2)}) copy-start(f32[1536]{0:T(1024)} %param.10) | copy-start | bytes 18436
  23.6 79.9 %all-gather.5.cloned.1.call-start = ((), (), s32[]{:S(2)}) async-start(), calls=%async_computation | async-start | bytes 4976640 | tf_op jit(solution)/shard_map/all_gather | solution.py:63
  24.3 437.7 %all-reduce.2.cloned.1.call-start = ((), (), s32[]{:S(2)}) async-start(), calls=%async_computation.2 | async-start | bytes 4423680 | tf_op jit(solution)/shard_map/psum | solution.py:80
  114.5 11.1 %copy-start.3 = (f32[8,720,48]{1,2,0:T(8,128)S(1)}, f32[8,720,48]{1,2,0:T(8,128)}, u32[]{:S(2)}) copy-start(f32[8,720,48]{1,2,0:T(8,128)} %get-tuple-element.262) | copy-start | bytes 3317764 | tf_op jit(solution)/shard_map/while
  125.6 9.2 %copy-start.6 = (f32[8,720]{1,0:T(8,128)S(1)}, f32[8,720]{1,0:T(8,128)}, u32[]{:S(2)}) copy-start(f32[8,720]{1,0:T(8,128)} %select_maximum_fusion.2) | copy-start | bytes 69124 | tf_op jit(solution)/shard_map/while
  134.8 1.0 copy-start.4
  147.6 11.2 %copy-start.3 = (f32[8,720,48]{1,2,0:T(8,128)S(1)}, f32[8,720,48]{1,2,0:T(8,128)}, u32[]{:S(2)}) copy-start(f32[8,720,48]{1,2,0:T(8,128)} %get-tuple-element.262) | copy-start | bytes 3317764 | tf_op jit(solution)/shard_map/while
  158.7 9.2 %copy-start.6 = (f32[8,720]{1,0:T(8,128)S(1)}, f32[8,720]{1,0:T(8,128)}, u32[]{:S(2)}) copy-start(f32[8,720]{1,0:T(8,128)} %select_maximum_fusion.2) | copy-start | bytes 69124 | tf_op jit(solution)/shard_map/while
  167.9 1.0 copy-start.4
  180.7 11.2 %copy-start.3 = (f32[8,720,48]{1,2,0:T(8,128)S(1)}, f32[8,720,48]{1,2,0:T(8,128)}, u32[]{:S(2)}) copy-start(f32[8,720,48]{1,2,0:T(8,128)} %get-tuple-element.262) | copy-start | bytes 3317764 | tf_op jit(solution)/shard_map/while
  191.8 9.2 %copy-start.6 = (f32[8,720]{1,0:T(8,128)S(1)}, f32[8,720]{1,0:T(8,128)}, u32[]{:S(2)}) copy-start(f32[8,720]{1,0:T(8,128)} %select_maximum_fusion.2) | copy-start | bytes 69124 | tf_op jit(solution)/shard_map/while
  213.8 11.2 %copy-start.3 = (f32[8,720,48]{1,2,0:T(8,128)S(1)}, f32[8,720,48]{1,2,0:T(8,128)}, u32[]{:S(2)}) copy-start(f32[8,720,48]{1,2,0:T(8,128)} %get-tuple-element.262) | copy-start | bytes 3317764 | tf_op jit(solution)/shard_map/while
  225.0 9.2 %copy-start.6 = (f32[8,720]{1,0:T(8,128)S(1)}, f32[8,720]{1,0:T(8,128)}, u32[]{:S(2)}) copy-start(f32[8,720]{1,0:T(8,128)} %select_maximum_fusion.2) | copy-start | bytes 69124 | tf_op jit(solution)/shard_map/while
  246.9 11.2 %copy-start.3 = (f32[8,720,48]{1,2,0:T(8,128)S(1)}, f32[8,720,48]{1,2,0:T(8,128)}, u32[]{:S(2)}) copy-start(f32[8,720,48]{1,2,0:T(8,128)} %get-tuple-element.262) | copy-start | bytes 3317764 | tf_op jit(solution)/shard_map/while
  258.1 9.2 %copy-start.6 = (f32[8,720]{1,0:T(8,128)S(1)}, f32[8,720]{1,0:T(8,128)}, u32[]{:S(2)}) copy-start(f32[8,720]{1,0:T(8,128)} %select_maximum_fusion.2) | copy-start | bytes 69124 | tf_op jit(solution)/shard_map/while
  267.2 1.0 copy-start.4
  280.0 11.2 %copy-start.3 = (f32[8,720,48]{1,2,0:T(8,128)S(1)}, f32[8,720,48]{1,2,0:T(8,128)}, u32[]{:S(2)}) copy-start(f32[8,720,48]{1,2,0:T(8,128)} %get-tuple-element.262) | copy-start | bytes 3317764 | tf_op jit(solution)/shard_map/while
  291.2 9.2 %copy-start.6 = (f32[8,720]{1,0:T(8,128)S(1)}, f32[8,720]{1,0:T(8,128)}, u32[]{:S(2)}) copy-start(f32[8,720]{1,0:T(8,128)} %select_maximum_fusion.2) | copy-start | bytes 69124 | tf_op jit(solution)/shard_map/while
  300.4 1.0 copy-start.4
  313.1 11.2 %copy-start.3 = (f32[8,720,48]{1,2,0:T(8,128)S(1)}, f32[8,720,48]{1,2,0:T(8,128)}, u32[]{:S(2)}) copy-start(f32[8,720,48]{1,2,0:T(8,128)} %get-tuple-element.262) | copy-start | bytes 3317764 | tf_op jit(solution)/shard_map/while
  324.3 9.2 %copy-start.6 = (f32[8,720]{1,0:T(8,128)S(1)}, f32[8,720]{1,0:T(8,128)}, u32[]{:S(2)}) copy-start(f32[8,720]{1,0:T(8,128)} %select_maximum_fusion.2) | copy-start | bytes 69124 | tf_op jit(solution)/shard_map/while
  333.5 1.0 copy-start.4
  346.2 11.2 %copy-start.3 = (f32[8,720,48]{1,2,0:T(8,128)S(1)}, f32[8,720,48]{1,2,0:T(8,128)}, u32[]{:S(2)}) copy-start(f32[8,720,48]{1,2,0:T(8,128)} %get-tuple-element.262) | copy-start | bytes 3317764 | tf_op jit(solution)/shard_map/while
  357.4 9.2 %copy-start.6 = (f32[8,720]{1,0:T(8,128)S(1)}, f32[8,720]{1,0:T(8,128)}, u32[]{:S(2)}) copy-start(f32[8,720]{1,0:T(8,128)} %select_maximum_fusion.2) | copy-start | bytes 69124 | tf_op jit(solution)/shard_map/while
  366.6 1.0 copy-start.4
  369.0 93.0 %copy-start.2 = (bf16[720,1536]{1,0:T(8,128)(2,1)S(1)}, bf16[720,1536]{1,0:T(8,128)(2,1)}, u32[]{:S(2)}) copy-start(bf16[720,1536]{1,0:T(8,128)(2,1)} %param.9) | copy-start | bytes 6635524
  371.7 93.7 %copy-start.8 = (f32[1536]{0:T(1024)S(1)}, f32[1536]{0:T(1024)}, u32[]{:S(2)}) copy-start(f32[1536]{0:T(1024)} %param.13) | copy-start | bytes 18436
  371.7 263.0 %all-gather.9.cloned.1.call-start = ((), (), s32[]{:S(2)}) async-start(), calls=%async_computation.3 | async-start | bytes 11059200 | tf_op jit(solution)/shard_map/all_gather | solution.py:11
  462.0 2.4 copy-start.5
  (2 other events, 2.0 us)
Sparse Core Ops, SparseCore 0:
  23.7 40.2 all-gather.6
  65.9 37.5 all-gather.4
  371.8 90.1 all-reduce.1
  478.5 156.1 all-gather.8
